TPU v7x, 32 devices: a whole 2x2x4 slice. The times are simulated.
32 devices in a mesh: section: 8 (over y, x, core), tp: 4 (over z).
Axes of the slice: x: 2, y: 2, z: 4, core: 2. Of those that a mesh axis runs over, the one named last changes fastest.
Arguments:
- stash: bfloat16 [8, 2, 256, 4096], P('section', None, 'tp'), may hold values from -660 to 660
- slot: int32 [8], P('section'), may hold values from 0 to 1
- doc_ids: int32 [8, 2, 256], P('section', None, 'tp'), may hold values from 0 to 3, never falling along the last dimension, each value on 1 to 128 neighbouring positions
- norm_gain: bfloat16 [4096], replicated, may hold values from 0.099609375 to 1.8984375
- w_query: bfloat16 [4096, 4096], P(None, 'tp'), may hold values from -21 to 21
- w_key: bfloat16 [4096, 1024], P(None, 'tp'), may hold values from -21 to 21
- value_weight: bfloat16 [4096, 1024], P(None, 'tp'), may hold values from -0.09375 to 0.09375
Outputs:
- received: bfloat16 [8, 256, 4096], P('section', None, 'tp')
Inputs may be any that keep to these rules, and one draw needn't show every extreme that they name: `doc_ids`: document numbers never fall along a micro-batch.
All inputs are finite; a program needn't handle non-finite values.
Results may differ from a plain program's by a relative error of at most 0.025.
The roundings to bfloat16 on the way count: a program that leaves them out, or rounds other values in their place, can miss the bound.
Values may be sent and summed in bfloat16 or wider, within the bound.
A program may use at most 64 MiB of HBM per device.

v0:
```python
import math

import jax
import jax.numpy as jnp
from jax import lax
from jax.sharding import PartitionSpec as P

HEAD_SIZE = 128


ROPE_BASE = 500000.0
NORM_EPSILON = 1e-05


def from_behind(block, axis, distance):
    devices = range(lax.axis_size(axis))
    route = [(i - distance, i) for i in devices if i - distance in devices]
    return lax.ppermute(block, axis, route)


def rotate(values, positions):
    head_width = values.shape[-1]
    half_width = head_width // 2
    freq_index = jnp.arange(half_width, dtype=jnp.float32)
    inverse = jnp.power(jnp.float32(ROPE_BASE), -2.0 * freq_index / head_width)
    angles = positions.astype(jnp.float32)[:, None] * inverse[None, :]
    cosine = jnp.concatenate([jnp.cos(angles), jnp.cos(angles)], -1)[:, None, :]
    sine_part = jnp.concatenate([jnp.sin(angles), jnp.sin(angles)], -1)[:, None, :]
    turned = jnp.concatenate([-values[..., half_width:], values[..., :half_width]], -1)
    return values * cosine + turned * sine_part


def normalize(stash_rows, norm_gain):
    widened = stash_rows.astype(jnp.float32)
    mean_square = jnp.mean(widened * widened, axis=-1, keepdims=True)
    return (widened * lax.rsqrt(mean_square + NORM_EPSILON) * norm_gain.astype(jnp.float32)).astype(
        jnp.bfloat16
    )


def project(normed, weight, positions, use_rope):
    length = normed.shape[0]
    product = jnp.dot(normed, weight, preferred_element_type=jnp.float32)
    if use_rope:
        product = rotate(product.reshape(length, -1, HEAD_SIZE), positions).reshape(length, -1)
    return product.astype(jnp.bfloat16)


def attend(queries, keys, values, doc_rows):
    length = queries.shape[0]
    kv_count = keys.shape[1] // HEAD_SIZE
    group_size = queries.shape[1] // HEAD_SIZE // kv_count
    grouped = queries.reshape(length, kv_count, group_size, HEAD_SIZE)
    key_heads = keys.reshape(length, kv_count, HEAD_SIZE)
    value_heads = values.reshape(length, kv_count, HEAD_SIZE)
    scores = jnp.einsum(
        "ihgd,jhd->hgij", grouped, key_heads, preferred_element_type=jnp.float32
    ) * (1.0 / math.sqrt(HEAD_SIZE))
    row_index = jnp.arange(length, dtype=jnp.int32)[:, None]
    col_index = jnp.arange(length, dtype=jnp.int32)[None, :]
    allowed = (col_index <= row_index) & (doc_rows[None, :] == doc_rows[:, None])
    scores = jnp.where(allowed, scores, -1e30)
    row_max = jnp.max(scores, axis=-1, keepdims=True)
    score_exponent = jnp.exp(scores - row_max)
    softmax_weights = (score_exponent / jnp.sum(score_exponent, axis=-1, keepdims=True)).astype(
        jnp.bfloat16
    )
    context = jnp.einsum(
        "hgij,jhd->ihgd", softmax_weights, value_heads, preferred_element_type=jnp.float32
    )
    return context.reshape(length, -1).astype(jnp.bfloat16)


def per_device(stash, slot, doc_ids, norm_gain, w_query, w_key, value_weight):
    group_count = lax.axis_size("tp")
    local_length = stash.shape[2]
    total_length = local_length * group_count
    chosen_slot = slot[0]
    picked = lax.dynamic_index_in_dim(stash[0], chosen_slot, 0, keepdims=False)
    doc_rows = lax.dynamic_index_in_dim(doc_ids[0], chosen_slot, 0, keepdims=False)
    doc_all = jnp.zeros((total_length,), jnp.int32)
    piece_rows = lax.all_gather(picked, "tp", axis=0, tiled=True)
    piece_docs = lax.all_gather(doc_rows, "tp", axis=0, tiled=True)
    piece_count = piece_rows.shape[0]
    positions = jnp.arange(piece_count, dtype=jnp.int32)
    normed = normalize(piece_rows, norm_gain)
    queries = project(normed, w_query, positions, True)
    keys = project(normed, w_key, positions, True)
    values = project(normed, value_weight, positions, False)
    doc_all = lax.dynamic_update_slice_in_dim(doc_all, piece_docs, jnp.int32(0), 0)
    queries, keys, values, doc_all = (queries, keys, values, doc_all)
    context = attend(queries, keys, values, doc_all)
    return from_behind(context[None], "section", 1)


def solution(mesh):
    placed = (
        P("section", None, "tp", None),
        P("section"),
        P("section", None, "tp"),
        P(),
        P(None, "tp"),
        P(None, "tp"),
        P(None, "tp"),
    )
    return jax.shard_map(
        per_device, mesh=mesh, in_specs=placed, out_specs=P("section", None, "tp"), check_vma=False
    )
```

profile of v0, /device:TPU:6, one launch (start us, length us, event | category | flops | bytes accessed | tf_op | source)
XLA Modules:
  0.0 91.9 jit_solution(12643340829580763346)
XLA Ops:
  6.5 0.0 copy-start
  6.5 0.0 copy-start.3
  6.5 0.0 copy-start.2
  6.5 0.0 all-gather.4.cloned.1.call-start
  7.3 1.9 %constant_dynamic-slice_fusion = bf16[1,1,64,4096]{3,2,1,0:T(8,128)(2,1)} fusion(bf16[1,2,64,4096]{3,2,1,0:T(8,128)(2,1)} %param.7, s32[]{:T(128)S(6)} %select_n.10), kind=kLoop, calls=%fused_computation.37 | loop fusion | bytes 1048580 | tf_op jit(solution)/shard_map/jit(dynamic_index_in_dim)/dynamic_slice | solution.py:79
  9.2 0.0 all-gather.4.cloned.1.call-update
  9.3 0.7 convert_element_type.52
  10.0 0.3 multiply_cosine_fusion
  10.3 0.1 copy.9
  10.4 0.1 copy.8
  10.5 0.0 copy-done.3
  10.5 0.6 dynamic-slice.2
  11.6 0.0 copy-done.2
  11.7 0.1 bitcast_dynamic-update-slice_fusion
  11.8 8.4 %all-reduce = s32[256]{0:T(256)S(1)} all-reduce(s32[256]{0:T(256)S(1)} %bitcast_dynamic-update-slice_fusion), channel_id=3, replica_groups=mesh['section'=8,'tp'=4] {'tp'}, use_global_device_ids=true, to_apply=%add | all-reduce | flops 256 | bytes 2048 | tf_op jit(solution)/shard_map/all_gather | solution.py:83
  20.2 0.1 fusion.12
  20.3 35.9 %all-gather.4.cloned.1.call-done = bf16[1,1,256,4096]{3,2,1,0:T(8,128)(2,1)} async-done(((bf16[1,1,64,4096]{3,2,1,0:T(8,128)(2,1)}), bf16[1,1,256,4096]{3,2,1,0:T(8,128)(2,1)}) %all-gather.4.cloned.1.call-update) | async-done | bytes 2097168 | tf_op jit(solution)/shard_map/all_gather | solution.py:82
  56.2 0.0 copy-start.1
  56.2 2.2 %fusion.1 = f32[256]{0:T(256)S(1)} fusion(bf16[1,1,256,4096]{3,2,1,0:T(8,128)(2,1)} %all-gather.4.cloned.1.call-done), kind=kLoop, calls=%fused_computation.3 | loop fusion | flops 3145472 | bytes 2098176 | tf_op jit(solution)/shard_map/reduce_sum | solution.py:35
  58.5 0.0 copy-done
  58.5 0.0 copy-done.1
  58.5 1.1 %fusion.23 = f32[256,256]{0,1:T(8,128)S(1)} fusion(bf16[4096,256]{1,0:T(8,128)(2,1)S(1)} %copy-done, bf16[1,1,256,4096]{3,2,1,0:T(8,128)(2,1)S(1)} %copy-done.1, f32[4096]{0:T(1024)S(1)} %convert_element_type.52, f32[256]{0:T(256)S(1)} %add_rsqrt_fusion), kind=kOutput, calls=%fused_computation.41 | convolution fusion | flops 541065216 | bytes 4473856 | tf_op jit(solution)/shard_map/dot_general | solution.py:43
  59.7 5.8 %fusion.21 = f32[256,1024]{1,0:T(8,128)S(1)} fusion(bf16[4096,1024]{1,0:T(8,128)(2,1)} %param.11, bf16[1,1,256,4096]{3,2,1,0:T(8,128)(2,1)S(1)} %copy-done.1, f32[4096]{0:T(1024)S(1)} %convert_element_type.52, f32[256]{0:T(256)S(1)} %add_rsqrt_fusion), kind=kOutput, calls=%fused_computation.40 | convolution fusion | flops 2151677952 | bytes 11551744 | tf_op jit(solution)/shard_map/dot_general | solution.py:43
  65.5 0.2 copy.20
  65.7 0.3 slice_negate_fusion
  66.1 0.4 maximum_multiply_fusion
  66.4 0.1 mul.129
  66.5 0.6 fusion.5
  67.1 0.4 reshape.69
  67.5 2.2 %fusion.26 = (f32[2,4,256]{2,1,0:T(4,128)S(1)}, f32[2,4,256,256]{2,3,1,0:T(8,128)}) fusion(pred[256,256]{0,1:T(8,128)(4,1)S(1)} %fusion.12, bf16[256,2,128,1]{0,2,3,1:T(8,128)(2,1)S(1)} %bitcast.66, bf16[256,2,4,128]{3,2,1,0:T(4,128)(2,1)S(1)} %reshape.69), kind=kOutput, calls=%fused_computation.42 | convolution fusion | flops 136315136 | bytes 2826240 | tf_op jit(solution)/shard_map/sub | solution.py:64
  69.7 0.0 copy-start.4
  69.7 3.5 %convolution_convert_fusion.1 = bf16[256,256]{0,1:T(8,128)(2,1)S(1)} fusion(bf16[4096,256]{1,0:T(8,128)(2,1)} %param.13, bf16[1,1,256,4096]{3,2,1,0:T(8,128)(2,1)} %all-gather.4.cloned.1.call-done, f32[4096]{0:T(1024)S(1)} %convert_element_type.52, f32[256]{0:T(256)S(1)} %add_rsqrt_fusion), kind=kOutput, calls=%fused_computation.11 | convolution fusion | flops 541130752 | bytes 4342784 | tf_op jit(solution)/shard_map/dot_general | solution.py:43
  73.2 0.0 copy-done.4
  73.2 0.3 convolution_convert_fusion
  73.5 0.2 copy.13
  73.7 1.9 %collective-permute-start = (bf16[1,256,1024]{2,1,0:T(8,128)(2,1)S(1)}, bf16[1,256,1024]{2,1,0:T(8,128)(2,1)S(1)}, u32[]{:S(2)}, u32[]{:S(2)}) collective-permute-start(bf16[1,256,1024]{2,1,0:T(8,128)(2,1)S(1)} %copy.13), channel_id=1, source_target_pairs={{0,4},{4,8},{8,12},{12,16},{16,20},{20,24},{24,28},{1,5},{5,9},{9,... | collective-permute-start | bytes 1572872 | tf_op jit(solution)/shard_map/ppermute | solution.py:18
  75.7 8.6 %collective-permute-done = bf16[1,256,1024]{2,1,0:T(8,128)(2,1)S(1)} collective-permute-done((bf16[1,256,1024]{2,1,0:T(8,128)(2,1)S(1)}, bf16[1,256,1024]{2,1,0:T(8,128)(2,1)S(1)}, u32[]{:S(2)}, u32[]{:S(2)}) %collective-permute-start) | collective-permute-done | bytes 524320 | tf_op jit(solution)/shard_map/ppermute | solution.py:18
  84.2 0.8 copy.37
  (8 shorter events, 0.1 us)
Async XLA Ops:
  6.5 51.9 %copy-start = (bf16[4096,256]{1,0:T(8,128)(2,1)S(1)}, bf16[4096,256]{1,0:T(8,128)(2,1)}, u32[]{:S(2)}) copy-start(bf16[4096,256]{1,0:T(8,128)(2,1)} %param.12) | copy-start | bytes 6291460
  6.5 4.0 %copy-start.3 = (u32[32]{0:T(128)S(1)}, u32[32]{0:T(128)}, u32[]{:S(2)}) copy-start(u32[32]{0:T(128)} %constant.37) | copy-start | bytes 388
  6.5 5.1 %copy-start.2 = (s32[1,2,64]{2,1,0:T(2,128)S(1)}, s32[1,2,64]{2,1,0:T(2,128)}, u32[]{:S(2)}) copy-start(s32[1,2,64]{2,1,0:T(2,128)} %param.9) | copy-start | bytes 1540
  6.5 49.7 %all-gather.4.cloned.1.call-start = ((), (), s32[]{:S(2)}) async-start(), calls=%async_computation | async-start | bytes 2621440 | tf_op jit(solution)/shard_map/all_gather | solution.py:82
  56.2 2.3 %copy-start.1 = (bf16[1,1,256,4096]{3,2,1,0:T(8,128)(2,1)S(1)}, bf16[1,1,256,4096]{3,2,1,0:T(8,128)(2,1)}, u32[]{:S(2)}) copy-start(bf16[1,1,256,4096]{3,2,1,0:T(8,128)(2,1)} %all-gather.4.cloned.1.call-done) | copy-start | bytes 6291460
  69.7 3.5 %copy-start.4 = (f32[2,4,256,256]{2,3,1,0:T(8,128)S(1)}, f32[2,4,256,256]{2,3,1,0:T(8,128)}, u32[]{:S(2)}) copy-start(f32[2,4,256,256]{2,3,1,0:T(8,128)} %get-tuple-element.12) | copy-start | bytes 6291460
  73.7 10.5 %collective-permute-start = (bf16[1,256,1024]{2,1,0:T(8,128)(2,1)S(1)}, bf16[1,256,1024]{2,1,0:T(8,128)(2,1)S(1)}, u32[]{:S(2)}, u32[]{:S(2)}) collective-permute-start(bf16[1,256,1024]{2,1,0:T(8,128)(2,1)S(1)} %copy.13), channel_id=1, source_target_pairs={{0,4},{4,8},{8,12},{12,16},{16,20},{20,24},{24,28},{1,5},{5,9},{9,... | collective-permute-start | bytes 1572872 | tf_op jit(solution)/shard_map/ppermute | solution.py:18
Sparse Core Ops, SparseCore 0:
  9.4 46.8 all-gather.3
where the time goes:
time: 93.1 us; the launch traced here: 91.9 us
  waiting for transfers between devices  44.5 us (48%)
  between operations  15 us (16%)
  matrix products  12.9 us (14%)
  blocking collectives  8.44 us (9%)
  other arithmetic  4.79 us (5%)
  local copies, waits for them, and re-layouts  4.37 us (5%)
  starting transfers between devices  1.92 us (2%)
    all_gather x1, waiting for transfers between devices, per_device(): piece_rows = lax.all_gather(picked, 'tp', axis=0, tiled=True)  35.9 us
    dot_general x3, matrix products, project(): product = jnp.dot(normed, weight, preferred_element_type=jnp.float32)  10.4 us
    ppermute x1, waiting for transfers between devices, from_behind(): return lax.ppermute(block, axis, route)  8.57 us
    all_gather x1, blocking collectives, per_device(): piece_docs = lax.all_gather(doc_rows, 'tp', axis=0, tiled=True)  8.44 us
    reduce_sum x1, other arithmetic, normalize(): mean_square = jnp.mean(widened * widened, axis=-1, keepdims=True)  2.23 us
    sub x1, matrix products, attend(): score_exponent = jnp.exp(scores - row_max)  2.18 us
    ppermute x1, starting transfers between devices, from_behind(): return lax.ppermute(block, axis, route)  1.92 us
    dynamic_slice x1, local copies, waits for them, and re-layouts, per_device(): picked = lax.dynamic_index_in_dim(stash[0], chosen_slot, 0, keepdims=False)  1.87 us
  transfers between devices with their start and end apart: 2, of which 2 were waited for; matrix products, arithmetic and copies ran while one was open for 2% of the time, Pallas kernels for 0%

commit v1 on v0

v1 whole, which is shorter than its diff:
```python
import functools
import math

import jax
import jax.numpy as jnp
import numpy as np
from jax import lax
from jax.experimental import pallas as pl
from jax.experimental.pallas import tpu as pltpu
from jax.sharding import PartitionSpec as P

HEAD_SIZE = 128
ROPE_BASE = 500000.0
NORM_EPSILON = 1e-05
PIECES = 4
MESH = pl.DeviceIdType.MESH
ANY = pl.BlockSpec(memory_space=pl.ANY)
VMEM = pl.BlockSpec(memory_space=pltpu.VMEM)


def rope_tables(length):
    half = HEAD_SIZE // 2
    freq = np.arange(half, dtype=np.float32)
    inverse = np.power(np.float32(ROPE_BASE), np.float32(-2.0) * freq / np.float32(HEAD_SIZE)).astype(np.float32)
    angles = np.arange(length, dtype=np.float32)[:, None] * inverse[None, :]
    cos, sin = np.cos(angles), np.sin(angles)
    return (
        np.concatenate([cos, cos], -1).astype(np.float32),
        np.concatenate([-sin, sin], -1).astype(np.float32),
    )


def kernel(
    n, ns,
    slot_ref, stash_ref, doc_ref, gain_ref, cos_ref, sin_ref, wq_ref, wk_ref, wv_ref,
    out_ref,
    raw, mine, dmine, w, xbuf, dbuf, dcol, acc, q, k, v,
    raw_sem, w_sem, shift_send, right_send, left_send, recv,
    dshift_send, dright_send, dleft_send, drecv,
):
    me = lax.axis_index("tp")
    sec = lax.axis_index("section")
    slots, rows, width = raw.shape
    pieces = PIECES
    part = width // pieces
    nq, nk = wq_ref.shape[1], wk_ref.shape[1]
    total_n = w.shape[2]
    total = n * rows
    has_right, has_left = me + 1 < n, me > 0
    has_next, has_prev = sec + 1 < ns, sec > 0

    raw_copy = pltpu.make_async_copy(stash_ref.at[0], raw, raw_sem)
    raw_copy.start()

    bar = pltpu.get_barrier_semaphore()
    for cond, target in (
        (has_right, {"tp": me + 1}),
        (has_left, {"tp": me - 1}),
        (has_next, {"section": sec + 1}),
        (has_prev, {"section": sec - 1}),
    ):
        @pl.when(cond)
        def _():
            pl.semaphore_signal(bar, inc=1, device_id=target, device_id_type=MESH)

    def w_copies(p):
        span = pl.ds(pl.multiple_of(p * part, part), part)
        return (
            pltpu.make_async_copy(wq_ref.at[span], w.at[p, :, 0:nq], w_sem.at[p, 0]),
            pltpu.make_async_copy(wk_ref.at[span], w.at[p, :, nq:nq + nk], w_sem.at[p, 1]),
            pltpu.make_async_copy(wv_ref.at[span], w.at[p, :, nq + nk:total_n], w_sem.at[p, 2]),
        )

    @pl.when(has_prev)
    def _():
        for p in range(pieces):
            for c in w_copies(p):
                c.start()

    chosen = slot_ref[0]
    dmine[...] = jnp.zeros_like(dmine)
    docs = doc_ref[0, 0:1, :]
    for i in range(1, slots):
        docs = jnp.where(jnp.full(docs.shape, chosen, jnp.int32) == i, doc_ref[0, i:i + 1, :], docs)
    dmine[0:1, 0:rows] = docs
    raw_copy.wait()
    step = 16
    for r in range(0, rows, step):
        x = raw[0, r:r + step, :]
        for i in range(1, slots):
            x = jnp.where(jnp.full(x.shape, chosen, jnp.int32) == i, raw[i, r:r + step, :], x)
        x = x.astype(jnp.float32)
        scale = lax.rsqrt(jnp.mean(x * x, axis=-1, keepdims=True) + NORM_EPSILON)
        y = (x * scale * gain_ref[...].astype(jnp.float32)).astype(jnp.bfloat16)
        for p in range(pieces):
            mine[p, r:r + step, :] = y[:, p * part:(p + 1) * part]

    def edges(a):
        return a.astype(jnp.int32)

    pl.semaphore_wait(bar, edges(has_right) + edges(has_left) + edges(has_next) + edges(has_prev))

    def remote(src, dst, ss, rs, target):
        return pltpu.make_async_remote_copy(
            src_ref=src, dst_ref=dst, send_sem=ss, recv_sem=rs, device_id=target, device_id_type=MESH
        )

    def shift(p):
        return remote(mine.at[p], xbuf.at[me, p], shift_send.at[p], recv.at[me, p], {"section": sec + 1})

    def dshift():
        return remote(dmine, dbuf.at[me], dshift_send, drecv.at[me], {"section": sec + 1})

    def right(c, p):
        b = xbuf.at[c, p]
        return remote(b, b, right_send.at[c, p], recv.at[c, p], {"tp": me + 1})

    def left(c, p):
        b = xbuf.at[c, p]
        return remote(b, b, left_send.at[c, p], recv.at[c, p], {"tp": me - 1})

    def dright(c):
        b = dbuf.at[c]
        return remote(b, b, dright_send.at[c], drecv.at[c], {"tp": me + 1})

    def dleft(c):
        b = dbuf.at[c]
        return remote(b, b, dleft_send.at[c], drecv.at[c], {"tp": me - 1})

    @pl.when(has_next)
    def _():
        dshift().start()
        for p in range(pieces):
            shift(p).start()

    tile = 256

    def compute(c, p):
        x = xbuf[c, p]
        for t in range(0, total_n, tile):
            acc[c, :, t:t + tile] += jnp.dot(x, w[p, :, t:t + tile], preferred_element_type=jnp.float32)

        @pl.when(p == pieces - 1)
        def _():
            span = pl.ds(pl.multiple_of(c * rows, rows), rows)
            cos, sin = cos_ref[span, :], sin_ref[span, :]
            for h in range(0, nq + nk, HEAD_SIZE):
                u = acc[c, :, h:h + HEAD_SIZE]
                u = (u * cos + pltpu.roll(u, HEAD_SIZE // 2, 1) * sin).astype(jnp.bfloat16)
                if h < nq:
                    q[span, h:h + HEAD_SIZE] = u
                else:
                    k[span, h - nq:h - nq + HEAD_SIZE] = u
            v[span, :] = acc[c, :, nq + nk:total_n].astype(jnp.bfloat16)

    @pl.when(jnp.logical_not(has_prev))
    def _():
        out_ref[...] = jnp.zeros_like(out_ref)

    @pl.when(has_prev)
    def _():
        acc[...] = jnp.zeros_like(acc)


        dshift().wait_recv()

        @pl.when(has_right)
        def _():
            dright(me).start()

        @pl.when(has_left)
        def _():
            dleft(me).start()

        @pl.loop(0, pieces)
        def _(p):
            shift(p).wait_recv()

            @pl.when(has_right)
            def _():
                right(me, p).start()

            @pl.when(has_left)
            def _():
                left(me, p).start()

        @pl.loop(0, pieces)
        def _(p):
            for c in w_copies(p):
                c.wait()
            compute(me, p)

        @pl.loop(0, (n - 1) * pieces)
        def _(i):
            d, p = i // pieces + 1, i % pieces
            below, above = me - d, me + d

            @pl.when((below >= 0) & (p == 0))
            def _():
                dright(below).wait_recv()

                @pl.when(has_right)
                def _():
                    dright(below).start()

            @pl.when((above < n) & (p == 0))
            def _():
                dleft(above).wait_recv()

                @pl.when(has_left)
                def _():
                    dleft(above).start()

            @pl.when(below >= 0)
            def _():
                right(below, p).wait_recv()

                @pl.when(has_right)
                def _():
                    right(below, p).start()

            @pl.when(above < n)
            def _():
                left(above, p).wait_recv()

                @pl.when(has_left)
                def _():
                    left(above, p).start()

            @pl.when(below >= 0)
            def _():
                compute(below, p)

            @pl.when(above < n)
            def _():
                compute(above, p)

        pieces_row = [dbuf[c, 0:1, 0:rows] for c in range(n)]
        drow = jnp.concatenate(pieces_row, axis=1).astype(jnp.float32)
        lanes = dbuf.shape[2]
        for c in range(n):
            wide = jnp.broadcast_to(dbuf[c, 0:1, :].astype(jnp.float32), (lanes, lanes))
            dcol[c * rows:(c + 1) * rows, :] = wide.T[0:rows, :]

        group = (nq // HEAD_SIZE) // (nk // HEAD_SIZE)
        block = min(total, 256)
        factor = 1.0 / math.sqrt(HEAD_SIZE)
        for i in range(0, total, block):
            upto = i + block
            i_idx = lax.broadcasted_iota(jnp.int32, (block, upto), 0) + i
            j_idx = lax.broadcasted_iota(jnp.int32, (block, upto), 1)
            allowed = (j_idx <= i_idx) & (dcol[i:upto, 0:1] == drow[:, 0:upto])
            for h in range(nq // HEAD_SIZE):
                g = h // group
                scores = lax.dot_general(
                    q[i:upto, h * HEAD_SIZE:(h + 1) * HEAD_SIZE],
                    k[0:upto, g * HEAD_SIZE:(g + 1) * HEAD_SIZE],
                    (((1,), (1,)), ((), ())), preferred_element_type=jnp.float32,
                ) * factor
                scores = jnp.where(allowed, scores, -1e30)
                e = jnp.exp(scores - jnp.max(scores, axis=-1, keepdims=True))
                weights = (e * (1.0 / jnp.sum(e, axis=-1, keepdims=True))).astype(jnp.bfloat16)
                out_ref[0, i:upto, h * HEAD_SIZE:(h + 1) * HEAD_SIZE] = jnp.dot(
                    weights, v[0:upto, g * HEAD_SIZE:(g + 1) * HEAD_SIZE],
                    preferred_element_type=jnp.float32,
                ).astype(jnp.bfloat16)

        @pl.loop(0, n)
        def _(c):
            @pl.when(has_right & (c <= me))
            def _():
                dright(c).wait_send()
                for p in range(pieces):
                    right(c, p).wait_send()

            @pl.when(has_left & (c >= me))
            def _():
                dleft(c).wait_send()
                for p in range(pieces):
                    left(c, p).wait_send()

    @pl.when(has_next)
    def _():
        dshift().wait_send()
        for p in range(pieces):
            shift(p).wait_send()


def per_device(stash, slot, doc_ids, norm_gain, w_query, w_key, value_weight):
    n, ns = lax.axis_size("tp"), lax.axis_size("section")
    _, slots, rows, width = stash.shape
    total = n * rows
    nq, nk = w_query.shape[1], w_key.shape[1]
    total_n = nq + nk + value_weight.shape[1]
    cos, sin = rope_tables(total)
    lanes = -(-rows // 128) * 128
    bf, f32, dma = jnp.bfloat16, jnp.float32, pltpu.SemaphoreType.DMA
    part = width // PIECES
    return pl.pallas_call(
        functools.partial(kernel, n, ns),
        out_shape=jax.ShapeDtypeStruct((1, total, nq), bf),
        in_specs=[pl.BlockSpec(memory_space=pltpu.SMEM), ANY, VMEM, VMEM, VMEM, VMEM, ANY, ANY, ANY],
        out_specs=VMEM,
        scratch_shapes=[
            pltpu.VMEM((slots, rows, width), bf),
            pltpu.VMEM((PIECES, rows, part), bf),
            pltpu.VMEM((8, lanes), jnp.int32),
            pltpu.VMEM((PIECES, part, total_n), bf),
            pltpu.VMEM((n, PIECES, rows, part), bf),
            pltpu.VMEM((n, 8, lanes), jnp.int32),
            pltpu.VMEM((total, lanes), f32),
            pltpu.VMEM((n, rows, total_n), f32),
            pltpu.VMEM((total, nq), bf),
            pltpu.VMEM((total, nk), bf),
            pltpu.VMEM((total, nk), bf),
            dma,
            dma((PIECES, 3)),
            dma((PIECES,)),
            dma((n, PIECES)),
            dma((n, PIECES)),
            dma((n, PIECES)),
            dma,
            dma((n,)),
            dma((n,)),
            dma((n,)),
        ],
        compiler_params=pltpu.CompilerParams(collective_id=0, has_side_effects=True),
        cost_estimate=pl.CostEstimate(
            flops=2 * total * width * total_n, bytes_accessed=width * total_n * 2, transcendentals=0
        ),
    )(slot, stash, doc_ids, norm_gain[None], cos, sin, w_query, w_key, value_weight)


def solution(mesh):
    placed = (
        P("section", None, "tp", None),
        P("section"),
        P("section", None, "tp"),
        P(),
        P(None, "tp"),
        P(None, "tp"),
        P(None, "tp"),
    )
    return jax.shard_map(
        per_device, mesh=mesh, in_specs=placed, out_specs=P("section", None, "tp"), check_vma=False
    )
```

time: 93.1 us -> 48.4 us (0.52); the launches traced: 91.9 us -> 48.1 us
  waiting for transfers between devices: 44.5 us -> 0 us
  Pallas kernels: 0 us -> 44.3 us
  between operations: 15 us -> 0.66 us
  matrix products: 12.9 us -> 0 us
  blocking collectives: 8.44 us -> 0 us
  other arithmetic: 4.79 us -> 0 us
  starting transfers between devices: 1.92 us -> 0 us
  local copies, waits for them, and re-layouts: 4.37 us -> 3.18 us
    pallas_call x0 -> x1, Pallas kernels: none -> 44.3 us  [per_device(): pl.pallas_call(functools.partial(kernel, n, ns), out_shape=jax.ShapeDtype...]
    all_gather x1 -> x0, waiting for transfers between devices: 35.9 us -> none  [per_device(): piece_rows = lax.all_gather(picked, 'tp', axis=0, tiled=True)]
    dot_general x4 -> x0, matrix products: 10.7 us -> none  [the longest x3 10.4 us: project(): product = jnp.dot(normed, weight, preferred_element_type=jnp.float32)]
    ppermute x1 -> x0, waiting for transfers between devices: 8.57 us -> none  [from_behind(): return lax.ppermute(block, axis, route)]
    all_gather x1 -> x0, blocking collectives: 8.44 us -> none  [per_device(): piece_docs = lax.all_gather(doc_rows, 'tp', axis=0, tiled=True)]
    reduce_sum x1 -> x0, other arithmetic: 2.23 us -> none  [normalize(): mean_square = jnp.mean(widened * widened, axis=-1, keepdims=True)]
    sub x1 -> x0, matrix products: 2.18 us -> none  [attend(): score_exponent = jnp.exp(scores - row_max)]
    ppermute x1 -> x0, starting transfers between devices: 1.92 us -> none  [from_behind(): return lax.ppermute(block, axis, route)]
  transfers between devices with their start and end apart: 2 -> 0, of which waited for: 2 -> 0; matrix products, arithmetic and copies ran while one was open for 2% -> 0% of each run, Pallas kernels for 0% -> 0%
where the time goes in v1:
time: 48.4 us; the launch traced here: 48.1 us
  Pallas kernels  44.3 us (92%)
  local copies, waits for them, and re-layouts  3.18 us (7%)
  between operations  0.66 us (1%)
    pallas_call x1, Pallas kernels, per_device(): pl.pallas_call(functools.partial(kernel, n, ns), out_shape=jax.ShapeDtype...  44.3 us
    unnamed x1, local copies, waits for them, and re-layouts  1.87 us
    broadcast_in_dim x1, local copies, waits for them, and re-layouts, per_device(): norm_gain[None]  1.31 us

profile of v1, /device:TPU:6, one launch (start us, length us, event | category | flops | bytes accessed | tf_op | source)
XLA Modules:
  0.0 48.1 jit_solution(6721722629766930157)
XLA Ops:
  0.7 1.3 %broadcast_in_dim.3.gain_ref = bf16[1,4096]{1,0:T(2,128)(2,1)} reshape(bf16[4096]{0:T(1024)(128)(2,1)} %param.12) | data formatting | bytes 16384 | tf_op jit(solution)/shard_map/broadcast_in_dim | solution.py:331
  2.0 44.3 %shard_map.91 = bf16[1,256,1024]{2,1,0:T(8,128)(2,1)} custom-call(s32[1]{0:T(128)S(6)} %copy.11.slot_ref, bf16[1,2,64,4096]{3,2,1,0:T(8,128)(2,1)} %stash_ref.1, s32[1,2,64]{2,1,0:T(2,128)} %doc_ref.1, bf16[1,4096]{1,0:T(2,128)(2,1)} %broadcast_in_dim.3.gain_ref, f32[256,128]{1,0:T(8,128)} %constant.4.clone.cos_ref, f32[256,128]{1,0:T(8,128)} %constant.5.clone.sin_ref, ...), custom_call_target="tpu_custom_call" | custom-call | flops 3221225472 | bytes 12582912 | tf_op jit(solution)/shard_map/pallas_call | solution.py:299
  46.3 1.9 %copy.12 = bf16[1,256,1024]{2,1,0:T(8,128)(2,1)} copy(bf16[1,256,1024]{2,1,0:T(8,128)(2,1)} %shard_map.91) | data formatting | bytes 1048576

commit v2 on v1

--- a/solution.py
+++ b/solution.py
@@ -30,12 +30,19 @@
     )
 
 
+def early_pieces(sec, ns):
+    pairs = ns // 2
+    count = PIECES * jnp.maximum(pairs - 1 - sec // 2, 0) // pairs if pairs else 0 * sec
+    return jnp.where((sec % 2 == 1) & (sec + 1 < ns), count, 0)
+
+
 def kernel(
     n, ns,
     slot_ref, stash_ref, doc_ref, gain_ref, cos_ref, sin_ref, wq_ref, wk_ref, wv_ref,
-    out_ref,
-    raw, mine, dmine, w, xbuf, dbuf, dcol, acc, q, k, v,
+    q, k, v, dcol, drow,
+    raw, mine, dmine, w, xbuf, zbuf, dbuf, acc,
     raw_sem, w_sem, shift_send, right_send, left_send, recv,
+    zright_send, zleft_send, zrecv,
     dshift_send, dright_send, dleft_send, drecv,
 ):
     me = lax.axis_index("tp")
@@ -48,6 +55,7 @@
     total = n * rows
     has_right, has_left = me + 1 < n, me > 0
     has_next, has_prev = sec + 1 < ns, sec > 0
+    early, early_prev = early_pieces(sec, ns), early_pieces(sec - 1, ns)
 
     raw_copy = pltpu.make_async_copy(stash_ref.at[0], raw, raw_sem)
     raw_copy.start()
@@ -91,7 +99,7 @@
             x = jnp.where(jnp.full(x.shape, chosen, jnp.int32) == i, raw[i, r:r + step, :], x)
         x = x.astype(jnp.float32)
         scale = lax.rsqrt(jnp.mean(x * x, axis=-1, keepdims=True) + NORM_EPSILON)
-        y = (x * scale * gain_ref[...].astype(jnp.float32)).astype(jnp.bfloat16)
+        y = (x * scale * gain_ref[...].astype(jnp.float32)[None, :]).astype(jnp.bfloat16)
         for p in range(pieces):
             mine[p, r:r + step, :] = y[:, p * part:(p + 1) * part]
 
@@ -105,8 +113,17 @@
             src_ref=src, dst_ref=dst, send_sem=ss, recv_sem=rs, device_id=target, device_id_type=MESH
         )
 
+    def hop(src, c, p):
+        return remote(src, xbuf.at[c, p], shift_send.at[c, p], recv.at[c, p], {"section": sec + 1})
+
     def shift(p):
-        return remote(mine.at[p], xbuf.at[me, p], shift_send.at[p], recv.at[me, p], {"section": sec + 1})
+        return hop(mine.at[p], me, p)
+
+    def zright(src, c, p):
+        return remote(src, zbuf.at[c, p], zright_send.at[c, p], zrecv.at[c, p], {"tp": me + 1})
+
+    def zleft(src, c, p):
+        return remote(src, zbuf.at[c, p], zleft_send.at[c, p], zrecv.at[c, p], {"tp": me - 1})
 
     def dshift():
         return remote(dmine, dbuf.at[me], dshift_send, drecv.at[me], {"section": sec + 1})
@@ -132,15 +149,19 @@
         dshift().start()
         for p in range(pieces):
             shift(p).start()
+            for cond, make in ((has_right, zright), (has_left, zleft)):
+                @pl.when(cond & (p < early))
+                def _():
+                    make(mine.at[p], me, p).start()
 
     tile = 256
 
-    def compute(c, p):
+    def compute(c, p, last):
         x = xbuf[c, p]
         for t in range(0, total_n, tile):
             acc[c, :, t:t + tile] += jnp.dot(x, w[p, :, t:t + tile], preferred_element_type=jnp.float32)
 
-        @pl.when(p == pieces - 1)
+        @pl.when(last)
         def _():
             span = pl.ds(pl.multiple_of(c * rows, rows), rows)
             cos, sin = cos_ref[span, :], sin_ref[span, :]
@@ -153,15 +174,26 @@
                     k[span, h - nq:h - nq + HEAD_SIZE] = u
             v[span, :] = acc[c, :, nq + nk:total_n].astype(jnp.bfloat16)
 
-    @pl.when(jnp.logical_not(has_prev))
-    def _():
-        out_ref[...] = jnp.zeros_like(out_ref)
+    def own_forward():
+        @pl.loop(0, pieces)
+        def _(p):
+            @pl.when(has_right & (p >= early_prev))
+            def _():
+                right(me, p).start()
+
+            @pl.when(has_left & (p >= early_prev))
+            def _():
+                left(me, p).start()
+
+    def keep_docs(c):
+        drow[c] = dbuf[c]
+        lanes = dbuf.shape[2]
+        wide = jnp.broadcast_to(dbuf[c, 0:1, :].astype(jnp.float32), (lanes, lanes))
+        dcol[pl.ds(pl.multiple_of(c * rows, rows), rows), :] = wide.T[0:rows, :]
 
     @pl.when(has_prev)
     def _():
         acc[...] = jnp.zeros_like(acc)
-
-
         dshift().wait_recv()
 
         @pl.when(has_right)
@@ -171,29 +203,62 @@
         @pl.when(has_left)
         def _():
             dleft(me).start()
+
+        keep_docs(me)
 
         @pl.loop(0, pieces)
         def _(p):
             shift(p).wait_recv()
 
+        @pl.when(early == 0)
+        def _():
+            own_forward()
+
+    @pl.loop(0, (n - 1) * pieces)
+    def _(i):
+        d, p = i // pieces + 1, i % pieces
+        below, above = me - d, me + d
+        valid = p < early
+
+        @pl.when(valid & (below >= 0))
+        def _():
+            b = zbuf.at[below, p]
+            zright(b, below, p).wait_recv()
+
             @pl.when(has_right)
             def _():
-                right(me, p).start()
+                zright(b, below, p).start()
+
+            hop(b, below, p).start()
+
+        @pl.when(valid & (above < n))
+        def _():
+            b = zbuf.at[above, p]
+            zleft(b, above, p).wait_recv()
 
             @pl.when(has_left)
             def _():
-                left(me, p).start()
-
-        @pl.loop(0, pieces)
-        def _(p):
+                zleft(b, above, p).start()
+
+            hop(b, above, p).start()
+
+        @pl.when(has_prev & (i < pieces))
+        def _():
             for c in w_copies(p):
                 c.wait()
-            compute(me, p)
+            compute(me, p, p == pieces - 1)
+
+    @pl.when(has_prev)
+    def _():
+        @pl.when(early > 0)
+        def _():
+            own_forward()
 
         @pl.loop(0, (n - 1) * pieces)
         def _(i):
             d, p = i // pieces + 1, i % pieces
             below, above = me - d, me + d
+            late = p >= early_prev
 
             @pl.when((below >= 0) & (p == 0))
             def _():
@@ -203,6 +268,8 @@
                 def _():
                     dright(below).start()
 
+                keep_docs(below)
+
             @pl.when((above < n) & (p == 0))
             def _():
                 dleft(above).wait_recv()
@@ -211,7 +278,9 @@
                 def _():
                     dleft(above).start()
 
-            @pl.when(below >= 0)
+                keep_docs(above)
+
+            @pl.when(late & (below >= 0))
             def _():
                 right(below, p).wait_recv()
 
@@ -219,7 +288,7 @@
                 def _():
                     right(below, p).start()
 
-            @pl.when(above < n)
+            @pl.when(late & (above < n))
             def _():
                 left(above, p).wait_recv()
 
@@ -227,63 +296,99 @@
                 def _():
                     left(above, p).start()
 
-            @pl.when(below >= 0)
-            def _():
-                compute(below, p)
-
-            @pl.when(above < n)
-            def _():
-                compute(above, p)
-
-        pieces_row = [dbuf[c, 0:1, 0:rows] for c in range(n)]
-        drow = jnp.concatenate(pieces_row, axis=1).astype(jnp.float32)
-        lanes = dbuf.shape[2]
-        for c in range(n):
-            wide = jnp.broadcast_to(dbuf[c, 0:1, :].astype(jnp.float32), (lanes, lanes))
-            dcol[c * rows:(c + 1) * rows, :] = wide.T[0:rows, :]
-
-        group = (nq // HEAD_SIZE) // (nk // HEAD_SIZE)
-        block = min(total, 256)
-        factor = 1.0 / math.sqrt(HEAD_SIZE)
+            last = (p == pieces - 1) & (early_prev == 0)
+
+            @pl.when(late & (below >= 0))
+            def _():
+                compute(below, p, last)
+
+            @pl.when(late & (above < n))
+            def _():
+                compute(above, p, last)
+
+        @pl.loop(0, n * pieces)
+        def _(i):
+            c, p = i // pieces, i % pieces
+
+            @pl.when((c != me) & (p < early_prev))
+            def _():
+                hop(xbuf.at[c, p], c, p).wait_recv()
+                compute(c, p, p == early_prev - 1)
+
+        @pl.loop(0, n * pieces)
+        def _(i):
+            c, p = i // pieces, i % pieces
+
+            @pl.when(has_right & (c <= me) & (p == 0))
+            def _():
+                dright(c).wait_send()
+
+            @pl.when(has_left & (c >= me) & (p == 0))
+            def _():
+                dleft(c).wait_send()
+
+            @pl.when(has_right & (c <= me) & (p >= early_prev))
+            def _():
+                right(c, p).wait_send()
+
+            @pl.when(has_left & (c >= me) & (p >= early_prev))
+            def _():
+                left(c, p).wait_send()
+
+    @pl.when(has_next)
+    def _():
+        dshift().wait_send()
+
+        @pl.loop(0, n * pieces)
+        def _(i):
+            c, p = i // pieces, i % pieces
+
+            @pl.when((c == me) | (p < early))
+            def _():
+                hop(zbuf.at[c, p], c, p).wait_send()
+
+            @pl.when(has_right & (c <= me) & (p < early))
+            def _():
+                zright(zbuf.at[c, p], c, p).wait_send()
+
+            @pl.when(has_left & (c >= me) & (p < early))
+            def _():
+                zleft(zbuf.at[c, p], c, p).wait_send()
+
+
+def attend(n, rows, q, k, v, dcol, drow, out_ref):
+    sec = lax.axis_index("section")
+    g = pl.program_id(0)
+    total = n * rows
+    group = out_ref.shape[2] // HEAD_SIZE
+    block = 128 if total % 128 == 0 else total
+    factor = 1.0 / math.sqrt(HEAD_SIZE)
+
+    @pl.when(sec == 0)
+    def _():
+        out_ref[...] = jnp.zeros_like(out_ref)
+
+    @pl.when(sec > 0)
+    def _():
+        lane_docs = jnp.concatenate([drow[c, 0:1, 0:rows] for c in range(n)], axis=1).astype(jnp.float32)
+        cols = pl.ds(pl.multiple_of(g * HEAD_SIZE, HEAD_SIZE), HEAD_SIZE)
         for i in range(0, total, block):
             upto = i + block
             i_idx = lax.broadcasted_iota(jnp.int32, (block, upto), 0) + i
             j_idx = lax.broadcasted_iota(jnp.int32, (block, upto), 1)
-            allowed = (j_idx <= i_idx) & (dcol[i:upto, 0:1] == drow[:, 0:upto])
-            for h in range(nq // HEAD_SIZE):
-                g = h // group
+            allowed = (j_idx <= i_idx) & (dcol[i:upto, 0:1] == lane_docs[:, 0:upto])
+            for h in range(group):
+                wide = pl.ds(pl.multiple_of((g * group + h) * HEAD_SIZE, HEAD_SIZE), HEAD_SIZE)
                 scores = lax.dot_general(
-                    q[i:upto, h * HEAD_SIZE:(h + 1) * HEAD_SIZE],
-                    k[0:upto, g * HEAD_SIZE:(g + 1) * HEAD_SIZE],
+                    q[i:upto, wide], k[0:upto, cols],
                     (((1,), (1,)), ((), ())), preferred_element_type=jnp.float32,
                 ) * factor
                 scores = jnp.where(allowed, scores, -1e30)
                 e = jnp.exp(scores - jnp.max(scores, axis=-1, keepdims=True))
                 weights = (e * (1.0 / jnp.sum(e, axis=-1, keepdims=True))).astype(jnp.bfloat16)
                 out_ref[0, i:upto, h * HEAD_SIZE:(h + 1) * HEAD_SIZE] = jnp.dot(
-                    weights, v[0:upto, g * HEAD_SIZE:(g + 1) * HEAD_SIZE],
-                    preferred_element_type=jnp.float32,
+                    weights, v[0:upto, cols], preferred_element_type=jnp.float32,
                 ).astype(jnp.bfloat16)
-
-        @pl.loop(0, n)
-        def _(c):
-            @pl.when(has_right & (c <= me))
-            def _():
-                dright(c).wait_send()
-                for p in range(pieces):
-                    right(c, p).wait_send()
-
-            @pl.when(has_left & (c >= me))
-            def _():
-                dleft(c).wait_send()
-                for p in range(pieces):
-                    left(c, p).wait_send()
-
-    @pl.when(has_next)
-    def _():
-        dshift().wait_send()
-        for p in range(pieces):
-            shift(p).wait_send()
 
 
 def per_device(stash, slot, doc_ids, norm_gain, w_query, w_key, value_weight):
@@ -296,26 +401,32 @@
     lanes = -(-rows // 128) * 128
     bf, f32, dma = jnp.bfloat16, jnp.float32, pltpu.SemaphoreType.DMA
     part = width // PIECES
-    return pl.pallas_call(
+    q, k, v, dcol, drow = pl.pallas_call(
         functools.partial(kernel, n, ns),
-        out_shape=jax.ShapeDtypeStruct((1, total, nq), bf),
+        out_shape=(
+            jax.ShapeDtypeStruct((total, nq), bf),
+            jax.ShapeDtypeStruct((total, nk), bf),
+            jax.ShapeDtypeStruct((total, nk), bf),
+            jax.ShapeDtypeStruct((total, lanes), f32),
+            jax.ShapeDtypeStruct((n, 8, lanes), jnp.int32),
+        ),
         in_specs=[pl.BlockSpec(memory_space=pltpu.SMEM), ANY, VMEM, VMEM, VMEM, VMEM, ANY, ANY, ANY],
-        out_specs=VMEM,
+        out_specs=(VMEM,) * 5,
         scratch_shapes=[
             pltpu.VMEM((slots, rows, width), bf),
             pltpu.VMEM((PIECES, rows, part), bf),
             pltpu.VMEM((8, lanes), jnp.int32),
             pltpu.VMEM((PIECES, part, total_n), bf),
             pltpu.VMEM((n, PIECES, rows, part), bf),
+            pltpu.VMEM((n, PIECES, rows, part), bf),
             pltpu.VMEM((n, 8, lanes), jnp.int32),
-            pltpu.VMEM((total, lanes), f32),
             pltpu.VMEM((n, rows, total_n), f32),
-            pltpu.VMEM((total, nq), bf),
-            pltpu.VMEM((total, nk), bf),
-            pltpu.VMEM((total, nk), bf),
             dma,
             dma((PIECES, 3)),
-            dma((PIECES,)),
+            dma((n, PIECES)),
+            dma((n, PIECES)),
+            dma((n, PIECES)),
+            dma((n, PIECES)),
             dma((n, PIECES)),
             dma((n, PIECES)),
             dma((n, PIECES)),
@@ -328,7 +439,15 @@
         cost_estimate=pl.CostEstimate(
             flops=2 * total * width * total_n, bytes_accessed=width * total_n * 2, transcendentals=0
         ),
-    )(slot, stash, doc_ids, norm_gain[None], cos, sin, w_query, w_key, value_weight)
+    )(slot, stash, doc_ids, norm_gain, cos, sin, w_query, w_key, value_weight)
+    heads = nk // HEAD_SIZE
+    return pl.pallas_call(
+        functools.partial(attend, n, rows),
+        grid=(heads,),
+        out_shape=jax.ShapeDtypeStruct((1, total, nq), bf),
+        in_specs=[VMEM] * 5,
+        out_specs=pl.BlockSpec((1, total, nq // heads), lambda g: (0, 0, g)),
+    )(q, k, v, dcol, drow)
 
 
 def solution(mesh):

time: 48.4 us -> 51 us (1.054)
  the two profiles are of different devices: /device:TPU:6 before, /device:TPU:5 now
where the time goes in v2:
time: 51 us; the launch traced here: 50.8 us
  Pallas kernels  50.1 us (98%)
  between operations  0.66 us (1%)
    pallas_call x1, Pallas kernels, per_device(): pl.pallas_call(functools.partial(kernel, n, ns), out_shape=(jax.ShapeDtyp...  43.8 us
    pallas_call x1, Pallas kernels, per_device(): pl.pallas_call(functools.partial(attend, n, rows), grid=(heads,), out_sha...  6.32 us

profile of v2, /device:TPU:5, one launch (start us, length us, event | category | flops | bytes accessed | tf_op | source)
XLA Modules:
  0.0 50.8 jit_solution(14338739343537206790)
XLA Ops:
  0.7 43.8 %shard_map.91 = (bf16[256,1024]{1,0:T(8,128)(2,1)}, bf16[256,256]{1,0:T(8,128)(2,1)}, bf16[256,256]{1,0:T(8,128)(2,1)}, f32[256,128]{1,0:T(8,128)}, s32[4,8,128]{2,1,0:T(8,128)}) custom-call(s32[1]{0:T(128)S(6)} %copy.10.slot_ref, bf16[1,2,64,4096]{3,2,1,0:T(8,128)(2,1)} %stash_ref.1, s32[1,2,64]{2,1,0:T(2,128)} %doc_ref.1, bf16[4096]{0:T(1024)(128)(2,1)} %gain_ref.1, ...), custom_call_target="tpu_custom_call" | custom-call | flops 3221225472 | bytes 12582912 | tf_op jit(solution)/shard_map/pallas_call | solution.py:404
  44.4 6.3 %shard_map.92 = bf16[1,256,1024]{2,1,0:T(8,128)(2,1)} custom-call(bf16[256,1024]{1,0:T(8,128)(2,1)} %get-tuple-element.10.q, bf16[256,256]{1,0:T(8,128)(2,1)} %get-tuple-element.11.k, bf16[256,256]{1,0:T(8,128)(2,1)} %get-tuple-element.12.v, f32[256,128]{1,0:T(8,128)} %get-tuple-element.13.dcol, s32[4,8,128]{2,1,0:T(8,128)} %get-tuple-element.14.drow), custom_call_target="tpu_custom_call" | custom-call | tf_op jit(solution)/shard_map/pallas_call | solution.py:444

commit v3 on v2

--- a/solution.py
+++ b/solution.py
@@ -14,7 +14,9 @@
 NORM_EPSILON = 1e-05
 PIECES = 4
 MESH = pl.DeviceIdType.MESH
-ANY = pl.BlockSpec(memory_space=pl.ANY)
+GATHER_VMEM = 52 << 20
+ATTEND_VMEM = 24 << 20
+ANY = pl.BlockSpec(memory_space=pltpu.HBM)
 VMEM = pl.BlockSpec(memory_space=pltpu.VMEM)
 
 
@@ -210,56 +212,55 @@
         def _(p):
             shift(p).wait_recv()
 
-        @pl.when(early == 0)
-        def _():
-            own_forward()
-
-    @pl.loop(0, (n - 1) * pieces)
-    def _(i):
-        d, p = i // pieces + 1, i % pieces
-        below, above = me - d, me + d
-        valid = p < early
-
-        @pl.when(valid & (below >= 0))
-        def _():
-            b = zbuf.at[below, p]
-            zright(b, below, p).wait_recv()
-
-            @pl.when(has_right)
-            def _():
-                zright(b, below, p).start()
-
-            hop(b, below, p).start()
-
-        @pl.when(valid & (above < n))
-        def _():
-            b = zbuf.at[above, p]
-            zleft(b, above, p).wait_recv()
-
-            @pl.when(has_left)
-            def _():
-                zleft(b, above, p).start()
-
-            hop(b, above, p).start()
-
-        @pl.when(has_prev & (i < pieces))
-        def _():
+        own_forward()
+
+        @pl.loop(0, pieces)
+        def _(p):
             for c in w_copies(p):
                 c.wait()
             compute(me, p, p == pieces - 1)
 
+    def pass_early(d, p):
+        below, above = me - d, me + d
+
+        @pl.when(below >= 0)
+        def _():
+            b = zbuf.at[below, p]
+            zright(b, below, p).wait_recv()
+
+            @pl.when(has_right)
+            def _():
+                zright(b, below, p).start()
+
+            hop(b, below, p).start()
+
+        @pl.when(above < n)
+        def _():
+            b = zbuf.at[above, p]
+            zleft(b, above, p).wait_recv()
+
+            @pl.when(has_left)
+            def _():
+                zleft(b, above, p).start()
+
+            hop(b, above, p).start()
+
     @pl.when(has_prev)
     def _():
-        @pl.when(early > 0)
-        def _():
-            own_forward()
-
         @pl.loop(0, (n - 1) * pieces)
         def _(i):
             d, p = i // pieces + 1, i % pieces
             below, above = me - d, me + d
             late = p >= early_prev
 
+            @pl.when(p == 0)
+            def _():
+                @pl.loop(0, pieces)
+                def _(e):
+                    @pl.when(e < early)
+                    def _():
+                        pass_early(d, e)
+
             @pl.when((below >= 0) & (p == 0))
             def _():
                 dright(below).wait_recv()
@@ -356,13 +357,13 @@
                 zleft(zbuf.at[c, p], c, p).wait_send()
 
 
-def attend(n, rows, q, k, v, dcol, drow, out_ref):
+def attend(n, rows, q, k, v, dcol, drow, out_ref, s_buf, p_buf):
     sec = lax.axis_index("section")
     g = pl.program_id(0)
     total = n * rows
     group = out_ref.shape[2] // HEAD_SIZE
     block = 128 if total % 128 == 0 else total
-    factor = 1.0 / math.sqrt(HEAD_SIZE)
+    factor = math.log2(math.e) / math.sqrt(HEAD_SIZE)
 
     @pl.when(sec == 0)
     def _():
@@ -372,22 +373,33 @@
     def _():
         lane_docs = jnp.concatenate([drow[c, 0:1, 0:rows] for c in range(n)], axis=1).astype(jnp.float32)
         cols = pl.ds(pl.multiple_of(g * HEAD_SIZE, HEAD_SIZE), HEAD_SIZE)
-        for i in range(0, total, block):
+        vg = v[:, cols]
+        vg = jnp.concatenate([vg, jnp.ones_like(vg)], axis=1)
+        starts = range(0, total, block)
+        for i in starts:
             upto = i + block
+            keys = k[0:upto, cols]
             i_idx = lax.broadcasted_iota(jnp.int32, (block, upto), 0) + i
             j_idx = lax.broadcasted_iota(jnp.int32, (block, upto), 1)
             allowed = (j_idx <= i_idx) & (dcol[i:upto, 0:1] == lane_docs[:, 0:upto])
             for h in range(group):
                 wide = pl.ds(pl.multiple_of((g * group + h) * HEAD_SIZE, HEAD_SIZE), HEAD_SIZE)
-                scores = lax.dot_general(
-                    q[i:upto, wide], k[0:upto, cols],
-                    (((1,), (1,)), ((), ())), preferred_element_type=jnp.float32,
-                ) * factor
-                scores = jnp.where(allowed, scores, -1e30)
-                e = jnp.exp(scores - jnp.max(scores, axis=-1, keepdims=True))
-                weights = (e * (1.0 / jnp.sum(e, axis=-1, keepdims=True))).astype(jnp.bfloat16)
-                out_ref[0, i:upto, h * HEAD_SIZE:(h + 1) * HEAD_SIZE] = jnp.dot(
-                    weights, v[0:upto, cols], preferred_element_type=jnp.float32,
+                raw = lax.dot_general(
+                    q[i:upto, wide], keys, (((1,), (1,)), ((), ())), preferred_element_type=jnp.float32
+                )
+                s_buf[h, i:upto, 0:upto] = jnp.where(allowed, raw, -1e30)
+        for i in starts:
+            upto = i + block
+            for h in range(group):
+                x = s_buf[h, i:upto, 0:upto]
+                e = jnp.exp2((x - jnp.max(x, axis=-1, keepdims=True)) * factor)
+                p_buf[h, i:upto, 0:upto] = e.astype(jnp.bfloat16)
+        for i in starts:
+            upto = i + block
+            for h in range(group):
+                both = jnp.dot(p_buf[h, i:upto, 0:upto], vg[0:upto], preferred_element_type=jnp.float32)
+                out_ref[0, i:upto, h * HEAD_SIZE:(h + 1) * HEAD_SIZE] = (
+                    both[:, 0:HEAD_SIZE] / both[:, HEAD_SIZE:]
                 ).astype(jnp.bfloat16)
 
 
@@ -435,7 +447,9 @@
             dma((n,)),
             dma((n,)),
         ],
-        compiler_params=pltpu.CompilerParams(collective_id=0, has_side_effects=True),
+        compiler_params=pltpu.CompilerParams(
+            collective_id=0, has_side_effects=True, vmem_limit_bytes=GATHER_VMEM
+        ),
         cost_estimate=pl.CostEstimate(
             flops=2 * total * width * total_n, bytes_accessed=width * total_n * 2, transcendentals=0
         ),
@@ -447,6 +461,11 @@
         out_shape=jax.ShapeDtypeStruct((1, total, nq), bf),
         in_specs=[VMEM] * 5,
         out_specs=pl.BlockSpec((1, total, nq // heads), lambda g: (0, 0, g)),
+        scratch_shapes=[
+            pltpu.VMEM((nq // nk, total, total), f32),
+            pltpu.VMEM((nq // nk, total, total), bf),
+        ],
+        compiler_params=pltpu.CompilerParams(vmem_limit_bytes=ATTEND_VMEM),
     )(q, k, v, dcol, drow)
 
 

time: 51 us -> 47.2 us (0.925)
  the two profiles are of different devices: /device:TPU:5 before, /device:TPU:6 now
where the time goes in v3:
time: 47.2 us; the launch traced here: 47 us
  Pallas kernels  43.1 us (91%)
  local copies, waits for them, and re-layouts  3.18 us (7%)
  between operations  0.67 us (1%)
    pallas_call x1, Pallas kernels, per_device(): pl.pallas_call(functools.partial(kernel, n, ns), out_shape=(jax.ShapeDtyp...  41 us
    unnamed x8, local copies, waits for them, and re-layouts  3.18 us
    pallas_call x1, Pallas kernels, per_device(): pl.pallas_call(functools.partial(attend, n, rows), grid=(heads,), out_sha...  2.15 us

profile of v3, /device:TPU:6, one launch (start us, length us, event | category | flops | bytes accessed | tf_op | source)
XLA Modules:
  0.0 47.0 jit_solution(10357165277071690068)
XLA Ops:
  0.7 0.0 copy-start
  0.7 0.9 %copy-done = f32[256,128]{1,0:T(8,128)S(1)} copy-done((f32[256,128]{1,0:T(8,128)S(1)}, f32[256,128]{1,0:T(8,128)}, u32[]{:S(2)}) %copy-start) | copy-done | bytes 131096
  1.6 0.0 copy-start.1
  1.6 0.9 %copy-done.1 = f32[256,128]{1,0:T(8,128)S(1)} copy-done((f32[256,128]{1,0:T(8,128)S(1)}, f32[256,128]{1,0:T(8,128)}, u32[]{:S(2)}) %copy-start.1) | copy-done | bytes 131096
  2.5 0.0 copy-start.2
  2.5 0.7 %copy-done.2 = bf16[4096]{0:T(1024)(128)(2,1)S(1)} copy-done((bf16[4096]{0:T(1024)(128)(2,1)S(1)}, bf16[4096]{0:T(1024)(128)(2,1)}, u32[]{:S(2)}) %copy-start.2) | copy-done | bytes 8216
  3.2 0.0 copy-start.3
  3.2 0.7 %copy-done.3 = s32[1,2,64]{2,1,0:T(2,128)S(1)} copy-done((s32[1,2,64]{2,1,0:T(2,128)S(1)}, s32[1,2,64]{2,1,0:T(2,128)}, u32[]{:S(2)}) %copy-start.3) | copy-done | bytes 536
  3.8 41.0 %shard_map.91 = (bf16[256,1024]{1,0:T(8,128)(2,1)S(1)}, bf16[256,256]{1,0:T(8,128)(2,1)S(1)}, bf16[256,256]{1,0:T(8,128)(2,1)S(1)}, f32[256,128]{1,0:T(8,128)S(1)}, s32[4,8,128]{2,1,0:T(8,128)S(1)}) custom-call(s32[1]{0:T(128)S(6)} %copy.10.slot_ref, bf16[1,2,64,4096]{3,2,1,0:T(8,128)(2,1)} %stash_ref.1, s32[1,2,64]{2,1,0:T(2,128)S(1)} %copy-done.3, ...), custom_call_target="tpu_custom_call" | custom-call | flops 3221225472 | bytes 12582912 | tf_op jit(solution)/shard_map/pallas_call | solution.py:416
  44.8 2.2 %shard_map.92 = bf16[1,256,1024]{2,1,0:T(8,128)(2,1)} custom-call(bf16[256,1024]{1,0:T(8,128)(2,1)S(1)} %get-tuple-element.10.q, bf16[256,256]{1,0:T(8,128)(2,1)S(1)} %get-tuple-element.11.k, bf16[256,256]{1,0:T(8,128)(2,1)S(1)} %get-tuple-element.12.v, f32[256,128]{1,0:T(8,128)S(1)} %get-tuple-element.13.dcol, s32[4,8,128]{2,1,0:T(8,128)S(1)} %get-tuple-element.14.drow), custom_call_target="tpu_custom_call" | custom-call | tf_op jit(solution)/shard_map/pallas_call | solution.py:458
Async XLA Ops:
  0.7 0.9 %copy-start = (f32[256,128]{1,0:T(8,128)S(1)}, f32[256,128]{1,0:T(8,128)}, u32[]{:S(2)}) copy-start(f32[256,128]{1,0:T(8,128)} %constant.5.clone.sin_ref) | copy-start | bytes 393220
  1.6 0.9 %copy-start.1 = (f32[256,128]{1,0:T(8,128)S(1)}, f32[256,128]{1,0:T(8,128)}, u32[]{:S(2)}) copy-start(f32[256,128]{1,0:T(8,128)} %constant.4.clone.cos_ref) | copy-start | bytes 393220
  2.5 0.7 %copy-start.2 = (bf16[4096]{0:T(1024)(128)(2,1)S(1)}, bf16[4096]{0:T(1024)(128)(2,1)}, u32[]{:S(2)}) copy-start(bf16[4096]{0:T(1024)(128)(2,1)} %gain_ref.1) | copy-start | bytes 24580
  3.2 0.7 %copy-start.3 = (s32[1,2,64]{2,1,0:T(2,128)S(1)}, s32[1,2,64]{2,1,0:T(2,128)}, u32[]{:S(2)}) copy-start(s32[1,2,64]{2,1,0:T(2,128)} %doc_ref.1) | copy-start | bytes 1540

commit v4 on v3

--- a/solution.py
+++ b/solution.py
@@ -14,8 +14,8 @@
 NORM_EPSILON = 1e-05
 PIECES = 4
 MESH = pl.DeviceIdType.MESH
-GATHER_VMEM = 52 << 20
-ATTEND_VMEM = 24 << 20
+GATHER_VMEM = 60 << 20
+ATTEND_VMEM = 60 << 20
 ANY = pl.BlockSpec(memory_space=pltpu.HBM)
 VMEM = pl.BlockSpec(memory_space=pltpu.VMEM)
 
@@ -40,12 +40,13 @@
 
 def kernel(
     n, ns,
-    slot_ref, stash_ref, doc_ref, gain_ref, cos_ref, sin_ref, wq_ref, wk_ref, wv_ref,
+    slot_ref, stash_ref, doc_hbm, gain_hbm, cos_hbm, sin_hbm, wq_ref, wk_ref, wv_ref,
     q, k, v, dcol, drow,
     raw, mine, dmine, w, xbuf, zbuf, dbuf, acc,
     raw_sem, w_sem, shift_send, right_send, left_send, recv,
     zright_send, zleft_send, zrecv,
     dshift_send, dright_send, dleft_send, drecv,
+    doc_ref, gain_ref, cos_ref, sin_ref, small_sem,
 ):
     me = lax.axis_index("tp")
     sec = lax.axis_index("section")
@@ -61,6 +62,14 @@
 
     raw_copy = pltpu.make_async_copy(stash_ref.at[0], raw, raw_sem)
     raw_copy.start()
+    small = [
+        pltpu.make_async_copy(src, dst, small_sem.at[i])
+        for i, (src, dst) in enumerate(
+            ((gain_hbm, gain_ref), (doc_hbm, doc_ref), (cos_hbm, cos_ref), (sin_hbm, sin_ref))
+        )
+    ]
+    for c in small:
+        c.start()
 
     bar = pltpu.get_barrier_semaphore()
     for cond, target in (
@@ -89,6 +98,8 @@
 
     chosen = slot_ref[0]
     dmine[...] = jnp.zeros_like(dmine)
+    for c in small:
+        c.wait()
     docs = doc_ref[0, 0:1, :]
     for i in range(1, slots):
         docs = jnp.where(jnp.full(docs.shape, chosen, jnp.int32) == i, doc_ref[0, i:i + 1, :], docs)
@@ -163,6 +174,9 @@
         for t in range(0, total_n, tile):
             acc[c, :, t:t + tile] += jnp.dot(x, w[p, :, t:t + tile], preferred_element_type=jnp.float32)
 
+        if last is False:
+            return
+
         @pl.when(last)
         def _():
             span = pl.ds(pl.multiple_of(c * rows, rows), rows)
@@ -245,6 +259,17 @@
 
             hop(b, above, p).start()
 
+    def take_early(below, above):
+        @pl.loop(0, 2 * pieces)
+        def _(i):
+            c = jnp.where(i < pieces, below, above)
+            p = i % pieces
+
+            @pl.when((c >= 0) & (c < n) & (p < early_prev))
+            def _():
+                hop(xbuf.at[c, p], c, p).wait_recv()
+                compute(c, p, False)
+
     @pl.when(has_prev)
     def _():
         @pl.loop(0, (n - 1) * pieces)
@@ -281,6 +306,12 @@
 
                 keep_docs(above)
 
+            final = p == pieces - 1
+
+            @pl.when(final & (d == n - 1))
+            def _():
+                take_early(below, above)
+
             @pl.when(late & (below >= 0))
             def _():
                 right(below, p).wait_recv()
@@ -297,24 +328,17 @@
                 def _():
                     left(above, p).start()
 
-            last = (p == pieces - 1) & (early_prev == 0)
+            @pl.when(final & (d < n - 1))
+            def _():
+                take_early(below, above)
 
             @pl.when(late & (below >= 0))
             def _():
-                compute(below, p, last)
+                compute(below, p, final)
 
             @pl.when(late & (above < n))
             def _():
-                compute(above, p, last)
-
-        @pl.loop(0, n * pieces)
-        def _(i):
-            c, p = i // pieces, i % pieces
-
-            @pl.when((c != me) & (p < early_prev))
-            def _():
-                hop(xbuf.at[c, p], c, p).wait_recv()
-                compute(c, p, p == early_prev - 1)
+                compute(above, p, final)
 
         @pl.loop(0, n * pieces)
         def _(i):
@@ -422,7 +446,7 @@
             jax.ShapeDtypeStruct((total, lanes), f32),
             jax.ShapeDtypeStruct((n, 8, lanes), jnp.int32),
         ),
-        in_specs=[pl.BlockSpec(memory_space=pltpu.SMEM), ANY, VMEM, VMEM, VMEM, VMEM, ANY, ANY, ANY],
+        in_specs=[pl.BlockSpec(memory_space=pltpu.SMEM)] + [ANY] * 8,
         out_specs=(VMEM,) * 5,
         scratch_shapes=[
             pltpu.VMEM((slots, rows, width), bf),
@@ -446,6 +470,11 @@
             dma((n,)),
             dma((n,)),
             dma((n,)),
+            pltpu.VMEM(doc_ids.shape, jnp.int32),
+            pltpu.VMEM(norm_gain.shape, bf),
+            pltpu.VMEM(cos.shape, f32),
+            pltpu.VMEM(sin.shape, f32),
+            dma((4,)),
         ],
         compiler_params=pltpu.CompilerParams(
             collective_id=0, has_side_effects=True, vmem_limit_bytes=GATHER_VMEM

time: 47.2 us -> 43.8 us (0.928)
  local copies, waits for them, and re-layouts: 3.18 us -> 0 us
    unnamed x8 -> x0, local copies, waits for them, and re-layouts: 3.18 us -> none
    pallas_call x1, Pallas kernels: 41 us -> 39.6 us  [per_device(): pl.pallas_call(functools.partial(kernel, n, ns), out_shape=(jax.ShapeDtyp...]
    pallas_call x1, Pallas kernels: 2.15 us -> 3.35 us  [per_device(): pl.pallas_call(functools.partial(attend, n, rows), grid=(heads,), out_sha...]
where the time goes in v4:
time: 43.8 us; the launch traced here: 43.6 us
  Pallas kernels  42.9 us (98%)
  between operations  0.66 us (2%)
    pallas_call x1, Pallas kernels, per_device(): pl.pallas_call(functools.partial(kernel, n, ns), out_shape=(jax.ShapeDtyp...  39.6 us
    pallas_call x1, Pallas kernels, per_device(): pl.pallas_call(functools.partial(attend, n, rows), grid=(heads,), out_sha...  3.35 us

profile of v4, /device:TPU:6, one launch (start us, length us, event | category | flops | bytes accessed | tf_op | source)
XLA Modules:
  0.0 43.6 jit_solution(1078872314114022729)
XLA Ops:
  0.7 39.6 %shard_map.91 = (bf16[256,1024]{1,0:T(8,128)(2,1)}, bf16[256,256]{1,0:T(8,128)(2,1)}, bf16[256,256]{1,0:T(8,128)(2,1)}, f32[256,128]{1,0:T(8,128)}, s32[4,8,128]{2,1,0:T(8,128)}) custom-call(s32[1]{0:T(128)S(6)} %copy.10.slot_ref, bf16[1,2,64,4096]{3,2,1,0:T(8,128)(2,1)} %stash_ref.1, s32[1,2,64]{2,1,0:T(2,128)} %doc_hbm.1, bf16[4096]{0:T(1024)(128)(2,1)} %gain_hbm.1, ...), custom_call_target="tpu_custom_call" | custom-call | flops 3221225472 | bytes 12582912 | tf_op jit(solution)/shard_map/pallas_call | solution.py:440
  40.2 3.3 %shard_map.92 = bf16[1,256,1024]{2,1,0:T(8,128)(2,1)} custom-call(bf16[256,1024]{1,0:T(8,128)(2,1)} %get-tuple-element.10.q, bf16[256,256]{1,0:T(8,128)(2,1)} %get-tuple-element.11.k, bf16[256,256]{1,0:T(8,128)(2,1)} %get-tuple-element.12.v, f32[256,128]{1,0:T(8,128)} %get-tuple-element.13.dcol, s32[4,8,128]{2,1,0:T(8,128)} %get-tuple-element.14.drow), custom_call_target="tpu_custom_call" | custom-call | tf_op jit(solution)/shard_map/pallas_call | solution.py:487
